TPU v7x, 256 devices: a whole 4x4x8 slice. The times are simulated.
256 devices in a mesh: shard: 32 (over z_lo, y, core), model: 8 (over z_hi, x).
Axes of the slice: x: 4, y: 4, z: 8 (z_hi: 2, z_lo: 4; z = z_hi * 4 + z_lo), core: 2. Of those that a mesh axis runs over, the one named last changes fastest.
Arguments:
- gradients: float32 [256, 128, 4096], P(None, 'shard', 'model'), may hold values from -6 to 6
- momentum: float32 [256, 128, 4096], P(None, 'shard', 'model'), may hold values from -6 to 6
- weights: float32 [256, 128, 4096], P(None, 'shard', 'model'), may hold values from -0.1875 to 0.1875
Outputs:
- new_weights: float32 [256, 128, 4096], P(None, 'shard', 'model')
- new_momentum: float32 [256, 128, 4096], P(None, 'shard', 'model')
All inputs are finite; a program needn't handle non-finite values.
Results may differ from a plain program's by a relative error of at most 0.00012.
Values sent between devices are 32-bit elements; how exact they have to be, the bound alone decides.
A program may use at most 64 MiB of HBM per device.

v0:
```python
import jax
import jax.numpy as jnp
from jax import lax
from jax.sharding import Mesh
from jax.sharding import PartitionSpec as P

ITERS = 4
SHARD = ("shard_0", "shard_1", "shard_2")


hold_rate = 0.9
learn_rate = 0.8


def in_blocks(array, dim, count):
    shape = array.shape
    parts = array.reshape(*shape[:dim], count, shape[dim] // count, *shape[dim + 1 :])
    return jnp.moveaxis(parts, dim, 0)


def in_order(parts, dim):
    parts = jnp.moveaxis(parts, 0, dim)
    shape = parts.shape
    return parts.reshape(*shape[:dim], shape[dim] * shape[dim + 1], *shape[dim + 2 :])


def turned_blocks(parts, axes, turns):
    inside = parts.shape[1:]
    filled = parts.reshape(*(lax.axis_size(a) for a in axes), *inside)
    for k in turns:
        filled = lax.all_to_all(filled, axes[k], k, k, tiled=True)
    return filled.reshape(-1, *inside)


def two_step_exchange(array, groups, turns, split_dim, concat_dim):
    count = lax.axis_size(groups[0]) * lax.axis_size(groups[1])
    parts = in_blocks(array, split_dim, count)
    return in_order(turned_blocks(parts, groups, turns), concat_dim)


def local(gradients, momentum, weights):
    new_momentum = hold_rate * momentum + gradients
    direction = hold_rate * new_momentum + gradients
    moved = two_step_exchange(direction, (("shard_0", "shard_1"), "shard_2"), (1, 0), 0, 1)
    whole = lax.all_to_all(moved, "model", split_axis=0, concat_axis=2, tiled=True)
    iterate = whole * lax.rsqrt(jnp.sum(whole * whole, axis=(1, 2), keepdims=True) + 1e-06)
    for step in range(ITERS):
        gram = jnp.einsum("mik,mjk->mij", iterate, iterate, precision=lax.Precision.HIGHEST)
        mixed = -4.775 * gram + 2.0315 * jnp.einsum(
            "mij,mjk->mik", gram, gram, precision=lax.Precision.HIGHEST
        )
        iterate = 3.4445 * iterate + jnp.einsum(
            "mij,mjk->mik", mixed, iterate, precision=lax.Precision.HIGHEST
        )
    iterate = lax.all_to_all(iterate, "model", split_axis=2, concat_axis=0, tiled=True)
    back = lax.all_to_all(iterate, SHARD, split_axis=1, concat_axis=0, tiled=True)
    new_weights = weights - learn_rate * back
    return (new_weights, new_momentum)


def solution(mesh):
    finer = Mesh(
        mesh.devices.reshape(4, 4, 2, mesh.shape["model"]),
        ("shard_0", "shard_1", "shard_2", "model"),
    )
    placed = (P(None, SHARD, "model"), P(None, SHARD, "model"), P(None, SHARD, "model"))
    return jax.shard_map(
        local,
        mesh=finer,
        in_specs=placed,
        out_specs=(P(None, SHARD, "model"), P(None, SHARD, "model")),
        check_vma=False,
    )
```

profile of v0, /device:TPU:32, one launch (start us, length us, event | category | flops | bytes accessed | tf_op | source)
XLA Modules:
  0.0 268.7 jit_solution(3068615582505055109)
XLA Ops:
  0.6 4.9 %fusion.3 = (f32[256,4,512]{2,0,1:T(8,128)}, f32[256,4,512]{2,0,1:T(8,128)S(1)}) fusion(f32[256,4,512]{2,1,0:T(4,128)} %param.4, f32[256,4,512]{2,1,0:T(4,128)} %param.3), kind=kLoop, calls=%fused_computation.9 | loop fusion | flops 2097152 | bytes 8388608 | tf_op jit(solution)/shard_map/add | solution.py:42
  5.5 1.8 copy.32
  7.3 5.4 %all_to_all.46 = f32[16,2,8,4,512]{4,3,2,0,1:T(4,128)S(1)} all-to-all(f32[16,2,8,4,512]{4,3,2,0,1:T(4,128)S(1)} %copy.32), channel_id=1, replica_groups=mesh['shard_0'=4,'shard_1'=4,'shard_2'=2,'model'=8] {'shard_2'}, dimensions={1} | all-to-all | bytes 4194304 | tf_op jit(solution)/shard_map/all_to_all | solution.py:31
  12.7 0.9 copy.33
  13.6 57.2 %all_to_all.47 = f32[16,2,8,4,512]{4,2,3,1,0:T(8,128)S(1)} all-to-all(f32[16,2,8,4,512]{4,2,3,1,0:T(8,128)S(1)} %copy.33), channel_id=1, replica_groups=mesh['shard_0'=4,'shard_1'=4,'shard_2'=2,'model'=8] {'shard_0','shard_1'}, dimensions={0} | all-to-all | bytes 4194304 | tf_op jit(solution)/shard_map/all_to_all | solution.py:31
  70.8 1.2 copy.44
  72.1 59.8 %all_to_all.48 = f32[8,128,512]{2,1,0:T(8,128)S(1)} all-to-all(f32[8,128,512]{2,1,0:T(8,128)S(1)} %copy.44), channel_id=1, replica_groups=mesh['shard_0'=4,'shard_1'=4,'shard_2'=2,'model'=8] {'model'}, dimensions={0} | all-to-all | bytes 4194304 | tf_op jit(solution)/shard_map/all_to_all | solution.py:45
  131.9 1.1 multiply_reduce_fusion
  133.7 1.8 fusion.5
  135.5 0.2 fusion.11
  135.7 2.7 %multiply_bitcast_fusion.1 = (f32[1,128,8,512]{3,1,2,0:T(8,128)}, f32[1,128,8,512]{3,1,2,0:T(8,128)}) fusion(f32[8,128,512]{2,1,0:T(8,128)S(1)} %all_to_all.48, f32[]{:T(128)S(6)} %rsqrt.4), kind=kLoop, calls=%fused_computation.14 | loop fusion | flops 1048576 | bytes 6291460 | tf_op jit(solution)/shard_map/mul | solution.py:46
  138.5 1.9 copy.36
  140.4 2.9 %copy.35 = f32[1,128,8,512]{1,3,2,0:T(8,128)} copy(f32[1,128,8,512]{3,1,2,0:T(8,128)} %get-tuple-element.9) | data formatting | bytes 4194304 | tf_op jit(solution)/shard_map/mul | solution.py:52
  143.3 2.9 %copy.37 = f32[128,4096]{1,0:T(8,128)} copy(f32[128,4096]{0,1:T(8,128)} %bitcast.61) | data formatting | bytes 4194304 | tf_op jit(solution)/shard_map/mul | solution.py:52
  146.2 3.6 %convolution_add_fusion.3 = f32[128,4096]{1,0:T(8,128)S(1)} fusion(f32[128,4096]{1,0:T(8,128)} %copy.37, f32[128,128]{1,0:T(8,128)S(1)} %fusion.11, f32[128,4096]{0,1:T(8,128)S(1)} %bitcast.57), kind=kOutput, calls=%fused_computation.4 | convolution fusion | flops 805830656 | bytes 6356992 | tf_op jit(solution)/shard_map/mij,mjk->mik/dot_general | solution.py:52
  149.8 1.8 fusion.13
  151.6 0.2 fusion.10
  151.8 2.0 convolution_add_fusion.2
  153.8 1.8 fusion.14
  155.6 0.2 fusion.9
  155.8 2.0 convolution_add_fusion.1
  157.9 1.8 fusion.15
  159.7 0.2 fusion.8
  159.9 2.3 fusion
  162.2 3.7 %copy.38 = f32[1,128,4096]{1,0,2:T(1,128)} copy(f32[1,128,4096]{2,1,0:T(8,128)S(1)} %fusion) | data formatting | bytes 4194304 | tf_op jit(solution)/shard_map/add | solution.py:52
  165.9 44.3 %all_to_all.49 = f32[1,128,4096]{1,0,2:T(1,128)S(1)} all-to-all(f32[1,128,4096]{1,0,2:T(1,128)} %copy.38), channel_id=1, replica_groups=mesh['shard_0'=4,'shard_1'=4,'shard_2'=2,'model'=8] {'model'}, dimensions={2} | all-to-all | bytes 4194304 | tf_op jit(solution)/shard_map/all_to_all | solution.py:55
  210.2 2.0 copy.45
  212.2 5.1 %all-to-all-start.4 = ((f32[8,128,512]{2,0,1:T(8,128)}), f32[8,128,512]{2,0,1:T(8,128)S(1)}, u32[]{:S(2)}, u32[]{:S(2)}) async-start(f32[8,128,512]{2,0,1:T(8,128)} %bitcast.59), calls=%async_computation.4 | async-start | bytes 4194304 | tf_op jit(solution)/shard_map/all_to_all | solution.py:56
  217.3 4.3 %copy.43 = f32[256,4,512]{2,1,0:T(4,128)} copy(f32[256,4,512]{2,0,1:T(8,128)} %get-tuple-element.6) | data formatting | bytes 4194304
  221.6 42.1 %all-to-all-done.4 = f32[8,128,512]{2,0,1:T(8,128)S(1)} async-done(((f32[8,128,512]{2,0,1:T(8,128)}), f32[8,128,512]{2,0,1:T(8,128)S(1)}, u32[]{:S(2)}, u32[]{:S(2)}) %all-to-all-start.4) | async-done | bytes 2097184 | tf_op jit(solution)/shard_map/all_to_all | solution.py:56
  263.7 0.0 copy-start
  263.7 0.2 broadcast_multiply_fusion
  263.9 1.3 copy-done
  265.3 0.7 bitcast_subtract_fusion
  266.0 2.7 copy.42
Async XLA Ops:
  212.2 51.5 %all-to-all-start.4 = ((f32[8,128,512]{2,0,1:T(8,128)}), f32[8,128,512]{2,0,1:T(8,128)S(1)}, u32[]{:S(2)}, u32[]{:S(2)}) async-start(f32[8,128,512]{2,0,1:T(8,128)} %bitcast.59), calls=%async_computation.4 | async-start | bytes 4194304 | tf_op jit(solution)/shard_map/all_to_all | solution.py:56
  263.7 1.6 copy-start
where the time goes:
time: 272 us; the launch traced here: 269 us
  blocking collectives  167 us (61%)
  waiting for transfers between devices  42.1 us (15%)
  local copies, waits for them, and re-layouts  25.6 us (9%)
  matrix products  17.9 us (7%)
  other arithmetic  9.74 us (4%)
  starting transfers between devices  5.06 us (2%)
    all_to_all x2, blocking collectives, turned_blocks(): filled = lax.all_to_all(filled, axes[k], k, k, tiled=True)  62.7 us
    all_to_all x1, blocking collectives, local(): lax.all_to_all(moved, 'model', split_axis=0, concat_axis=2, tiled=True)  59.8 us
    all_to_all x1, blocking collectives, local(): lax.all_to_all(iterate, 'model', split_axis=2, concat_axis=0, tiled=True)  44.3 us
    all_to_all x1, waiting for transfers between devices, local(): lax.all_to_all(iterate, SHARD, split_axis=1, concat_axis=0, tiled=True)  42.1 us
    dot_general x4, matrix products, local(): jnp.einsum('mij,mjk->mik', mixed, iterate, precision=lax.Precision.HIGHEST)  9.94 us
    unnamed x4, local copies, waits for them, and re-layouts  8.27 us
    dot_general x4, matrix products, local(): jnp.einsum('mik,mjk->mij', iterate, iterate, precision=lax.Precision.HIGH...  7.17 us
    mul x2, local copies, waits for them, and re-layouts, local(): 3.4445 * iterate  5.8 us
  transfers between devices with their start and end apart: 1, of which 1 were waited for; matrix products, arithmetic and copies ran while one was open for 2% of the time, Pallas kernels for 0%

commit v1 on v0

v1 whole, which is shorter than its diff:
```python
import functools

import jax
import jax.numpy as jnp
from jax import lax
from jax.experimental import pallas as pl
from jax.experimental.pallas import tpu as pltpu
from jax.sharding import PartitionSpec as P

MESH = pl.DeviceIdType.MESH
F32 = jnp.float32
ITERS = 4
ROUNDS = 2
PER = 4
hold_rate = 0.9
learn_rate = 0.8
HI = lax.Precision.HIGHEST


def dot(a, b):
    return lax.dot_general(a, b, (((1,), (0,)), ((), ())), precision=HI, preferred_element_type=F32)


def dot_t(a, b):
    return lax.dot_general(a, b, (((1,), (1,)), ((), ())), precision=HI, preferred_element_type=F32)


def merge_halves(a, b):
    low = lax.broadcasted_iota(jnp.int32, a.shape, 1) < 4
    return (
        jnp.where(low, a, pltpu.roll(b, 4, 1)),
        jnp.where(low, pltpu.roll(a, 4, 1), b),
    )


def kernel(
    g_hbm, m_hbm, back,
    gbuf, mbuf, D, R, X, G, GX, S, Z, QR, Y,
    gsem, msem, p1s, p1r, xs, xr, zs, zr, qs, qr, p2s, p2r, own1, own2,
):
    s, m = lax.axis_index("shard"), lax.axis_index("model")
    zl, yy, core = s // 8, (s // 2) % 4, s % 2
    zh, x = m // 4, m % 4
    side = zl // 2

    def group_of(d):
        z = d // 8
        return (zh * (3 - z) + (1 - zh) * z) * 8 + d % 8

    mine = group_of(s)
    partner = ((3 - zl) * 8 + s % 8, (1 - zh) * 4 + x)

    def dest(k):
        c, a, b = k // 16, (k % 16) // 4, k % 4
        z = side * a + (1 - side) * (3 - a)
        return z * 8 + ((yy + 2 + b) % 4) * 2 + c

    barrier = pltpu.get_barrier_semaphore()

    @pl.loop(1, 32)
    def _(k):
        pl.semaphore_signal(barrier, inc=1, device_id=((s + k) % 32, m), device_id_type=MESH)

    for k in range(1, 4):
        pl.semaphore_signal(barrier, inc=1, device_id=(s, zh * 4 + (x + k) % 4), device_id_type=MESH)
    pl.semaphore_signal(barrier, inc=1, device_id=partner, device_id_type=MESH)

    pieces, size = 4, 1024
    loads = []
    for i in range(pieces):
        part = pl.ds(i * size, size)
        loads.append((
            pltpu.make_async_copy(g_hbm.at[part], gbuf.at[part], gsem.at[i]),
            pltpu.make_async_copy(m_hbm.at[part], mbuf.at[part], msem.at[i]),
        ))
        loads[-1][0].start()
        loads[-1][1].start()
    for i in range(pieces):
        loads[i][0].wait()
        loads[i][1].wait()

        @pl.loop(0, size // 128)
        def _(b):
            rows = pl.ds(pl.multiple_of(i * size + b * 128, 128), 128)
            g = gbuf[rows, :]
            D[rows, :] = hold_rate * (hold_rate * mbuf[rows, :] + g) + g

    pl.semaphore_wait(barrier, 35)

    def p1_copy(r, d):
        t = group_of(d)
        return pltpu.make_async_remote_copy(
            src_ref=D.at[pl.ds(pl.multiple_of(t * 128 + r * 64, 64), 64), :],
            dst_ref=R.at[r, s // 2, s % 2],
            send_sem=p1s.at[r, d],
            recv_sem=p1r.at[r, s],
            device_id=(d, m),
            device_id_type=MESH,
        )

    def p1_from(r, q):
        return pltpu.make_async_remote_copy(
            src_ref=D.at[pl.ds(0, 64), :],
            dst_ref=R.at[r, q // 2, q % 2],
            send_sem=p1s.at[r, q],
            recv_sem=p1r.at[r, q],
            device_id=(q, m),
            device_id_type=MESH,
        )

    def p1_own(r):
        return pltpu.make_async_copy(
            D.at[pl.ds(pl.multiple_of(mine * 128 + r * 64, 64), 64), :], R.at[r, s // 2, s % 2], own1.at[r]
        )

    for r in range(ROUNDS):
        @pl.loop(0, 32)
        def _(k):
            d = dest(k)

            @pl.when(d != s)
            def _():
                p1_copy(r, d).start()

        p1_own(r).start()

    eye = (
        lax.broadcasted_iota(jnp.int32, (128, 128), 0) == lax.broadcasted_iota(jnp.int32, (128, 128), 1)
    ).astype(F32)

    def x_copy(r, to, slot):
        return pltpu.make_async_remote_copy(
            src_ref=G.at[r, to],
            dst_ref=GX.at[r, slot],
            send_sem=xs.at[r, to],
            recv_sem=xr.at[r, slot],
            device_id=(s, zh * 4 + to),
            device_id_type=MESH,
        )

    def q_copy(r, to, slot):
        return pltpu.make_async_remote_copy(
            src_ref=QR.at[r, slot],
            dst_ref=QR.at[r, slot],
            send_sem=qs.at[r, to],
            recv_sem=qr.at[r, slot],
            device_id=(s, zh * 4 + to),
            device_id_type=MESH,
        )

    def z_copy(r):
        return pltpu.make_async_remote_copy(
            src_ref=S.at[r], dst_ref=Z.at[r], send_sem=zs.at[r], recv_sem=zr.at[r],
            device_id=partner, device_id_type=MESH,
        )

    def p2_rows(t, r):
        return back.at[pl.ds(pl.multiple_of(t * 128 + r * 64, 64), 64), :]

    def p2_copy(r, d):
        return pltpu.make_async_remote_copy(
            src_ref=Y.at[r, d // 2, d % 2], dst_ref=p2_rows(mine, r), send_sem=p2s.at[r, d], recv_sem=p2r.at[r, s],
            device_id=(d, m), device_id_type=MESH,
        )

    def p2_from(r, q):
        return pltpu.make_async_remote_copy(
            src_ref=Y.at[r, q // 2, q % 2], dst_ref=p2_rows(group_of(q), r), send_sem=p2s.at[r, q],
            recv_sem=p2r.at[r, q], device_id=(q, m), device_id_type=MESH,
        )

    def p2_own(r):
        return pltpu.make_async_copy(Y.at[r, s // 2, s % 2], p2_rows(mine, r), own2.at[r])

    for r in range(ROUNDS):
        @pl.loop(1, 32)
        def _(k):
            p1_from(r, (s + k) % 32).wait_recv()

        p1_own(r).wait()

        @pl.loop(0, PER)
        def _(j):
            for h in range(2):
                rows = pl.ds(pl.multiple_of(j * 16 + h * 8, 8), 8)
                low, high = merge_halves(R[r, :, 0, rows, :], R[r, :, 1, rows, :])
                X[j, :, 256 * h : 256 * h + 128] = low.reshape(128, 128)
                X[j, :, 256 * h + 128 : 256 * h + 256] = high.reshape(128, 128)
            G[r, j] = dot_t(X[j], X[j])

        for k in range(1, 4):
            x_copy(r, (x + k) % 4, x).start()
        total = G[r, x]
        for k in range(1, 4):
            q = (x + k) % 4
            x_copy(r, q, q).wait_recv()
            total = total + GX[r, q]
        S[r] = total
        z_copy(r).start()
        z_copy(r).wait_recv()
        gram = S[r] + Z[r]
        scale = lax.rsqrt(jnp.sum(jnp.sum(gram * eye, axis=1, keepdims=True), axis=0, keepdims=True) + 1e-06)
        gram = gram * (scale * scale)
        factor = None
        for step in range(ITERS):
            mixed = 3.4445 * eye + (-4.775 * gram + 2.0315 * dot(gram, gram))
            factor = mixed if factor is None else dot(mixed, factor)
            if step < ITERS - 1:
                gram = dot(dot(mixed, gram), mixed)
        QR[r, x] = factor * scale
        for k in range(1, 4):
            q_copy(r, (x + k) % 4, x).start()
        for k in range(1, 4):
            q = (x + k) % 4
            q_copy(r, q, q).wait_recv()

        @pl.loop(0, PER)
        def _(j):
            for h in range(2):
                wide = dot(QR[r, j], X[j, :, 256 * h : 256 * h + 256])
                rows = pl.ds(pl.multiple_of(j * 16 + h * 8, 8), 8)
                even, odd = merge_halves(wide[:, :128].reshape(16, 8, 128), wide[:, 128:].reshape(16, 8, 128))
                Y[r, :, 0, rows, :] = even
                Y[r, :, 1, rows, :] = odd

        @pl.loop(0, 32)
        def _(k):
            d = dest(k)

            @pl.when(d != s)
            def _():
                p2_copy(r, d).start()

        p2_own(r).start()

    for r in range(ROUNDS):
        @pl.loop(1, 32)
        def _(k):
            q = (s + k) % 32
            p2_from(r, q).wait_recv()
            p1_copy(r, q).wait_send()
            p2_copy(r, q).wait_send()

        p2_own(r).wait()
        z_copy(r).wait_send()
        for k in range(1, 4):
            x_copy(r, (x + k) % 4, x).wait_send()
            q_copy(r, (x + k) % 4, x).wait_send()


def exchange(g, m):
    dma = pltpu.SemaphoreType.DMA
    return pl.pallas_call(
        kernel,
        out_shape=jax.ShapeDtypeStruct((4096, 128), F32),
        in_specs=[pl.BlockSpec(memory_space=pl.ANY)] * 2,
        out_specs=pl.BlockSpec(memory_space=pl.ANY),
        scratch_shapes=[
            pltpu.VMEM((4096, 128), F32),
            pltpu.VMEM((4096, 128), F32),
            pltpu.VMEM((4096, 128), F32),
            pltpu.VMEM((ROUNDS, 16, 2, 64, 128), F32),
            pltpu.VMEM((PER, 128, 512), F32),
            pltpu.VMEM((ROUNDS, PER, 128, 128), F32),
            pltpu.VMEM((ROUNDS, 4, 128, 128), F32),
            pltpu.VMEM((ROUNDS, 128, 128), F32),
            pltpu.VMEM((ROUNDS, 128, 128), F32),
            pltpu.VMEM((ROUNDS, 4, 128, 128), F32),
            pltpu.VMEM((ROUNDS, 16, 2, 64, 128), F32),
            dma((4,)), dma((4,)),
            dma((ROUNDS, 32)), dma((ROUNDS, 32)),
            dma((ROUNDS, 4)), dma((ROUNDS, 4)),
            dma((ROUNDS,)), dma((ROUNDS,)),
            dma((ROUNDS, 4)), dma((ROUNDS, 4)),
            dma((ROUNDS, 32)), dma((ROUNDS, 32)),
            dma((ROUNDS,)), dma((ROUNDS,)),
        ],
        compiler_params=pltpu.CompilerParams(
            collective_id=0, has_side_effects=True, vmem_limit_bytes=40 * 1024 * 1024
        ),
        name="exchange",
    )(g, m)


def flat(a):
    return a.reshape(256, 4, 4, 128).transpose(0, 2, 1, 3).reshape(4096, 128)


def unflat(a):
    return a.reshape(256, 4, 4, 128).transpose(0, 2, 1, 3).reshape(256, 4, 512)


def local(gradients, momentum, weights):
    g, m, w = flat(gradients), flat(momentum), flat(weights)
    back = exchange(g, m)
    new_momentum = hold_rate * m + g
    new_weights = w - learn_rate * back
    return (unflat(new_weights), unflat(new_momentum))


def solution(mesh):
    placed = P(None, "shard", "model")
    return jax.shard_map(
        local, mesh=mesh, in_specs=(placed,) * 3, out_specs=(placed, placed), check_vma=False
    )
```

time: 272 us -> 113 us (0.42)
  the two profiles are of different devices: /device:TPU:32 before, /device:TPU:1 now
where the time goes in v1:
time: 113 us
  Pallas kernels  105 us (93%)
  other arithmetic  3.6 us (3%)
  local copies, waits for them, and re-layouts  3.18 us (3%)
    pallas_call x1, Pallas kernels, exchange(): pl.pallas_call(kernel, out_shape=jax.ShapeDtypeStruct((4096, 128), F32),...  105 us
    unnamed x6, local copies, waits for them, and re-layouts  3.18 us

profile of v1, /device:TPU:1, one launch (start us, length us, event | category | flops | bytes accessed | tf_op | source)
XLA Modules:
  0.0 112.9 jit_solution(13805496470209297460)
XLA Ops:
  0.6 0.0 copy-start
  0.6 1.6 %copy-done = f32[256,4,512]{2,1,0:T(4,128)S(1)} copy-done((f32[256,4,512]{2,1,0:T(4,128)S(1)}, f32[256,4,512]{2,1,0:T(4,128)}, u32[]{:S(2)}) %copy-start) | copy-done | bytes 2097176
  2.2 0.0 copy-start.1
  2.2 1.6 %copy-done.1 = f32[256,4,512]{2,1,0:T(4,128)S(1)} copy-done((f32[256,4,512]{2,1,0:T(4,128)S(1)}, f32[256,4,512]{2,1,0:T(4,128)}, u32[]{:S(2)}) %copy-start.1) | copy-done | bytes 2097176
  3.8 0.0 copy-start.2
  3.8 105.5 %exchange.1 = f32[4096,128]{1,0:T(8,128)S(1)} custom-call(f32[4096,128]{1,0:T(8,128)S(1)} %bitcast.20, f32[4096,128]{1,0:T(8,128)S(1)} %bitcast.21), custom_call_target="tpu_custom_call" | custom-call | tf_op jit(solution)/shard_map/exchange/pallas_call | solution.py:253
  109.3 0.0 copy-done.2
  109.3 1.6 %multiply_subtract_fusion = f32[4096,128]{1,0:T(8,128)} fusion(f32[4096,128]{1,0:T(8,128)S(1)} %bitcast.22, f32[4096,128]{1,0:T(8,128)S(1)} %exchange.1), kind=kLoop, calls=%fused_computation.1 | loop fusion | flops 1048576 | bytes 6291456 | tf_op jit(solution)/shard_map/sub | solution.py:297
  110.9 2.0 %multiply_add_fusion = f32[256,4,512]{2,1,0:T(4,128)} fusion(f32[256,4,512]{2,1,0:T(4,128)S(1)} %copy-done, f32[256,4,512]{2,1,0:T(4,128)S(1)} %copy-done.1), kind=kLoop, calls=%fused_computation | loop fusion | flops 1048576 | bytes 6291456 | tf_op jit(solution)/shard_map/add | solution.py:296
Async XLA Ops:
  0.6 1.6 %copy-start = (f32[256,4,512]{2,1,0:T(4,128)S(1)}, f32[256,4,512]{2,1,0:T(4,128)}, u32[]{:S(2)}) copy-start(f32[256,4,512]{2,1,0:T(4,128)} %param.3) | copy-start | bytes 6291460
  2.2 1.6 %copy-start.1 = (f32[256,4,512]{2,1,0:T(4,128)S(1)}, f32[256,4,512]{2,1,0:T(4,128)}, u32[]{:S(2)}) copy-start(f32[256,4,512]{2,1,0:T(4,128)} %param.4) | copy-start | bytes 6291460
  3.8 105.5 %copy-start.2 = (f32[256,4,512]{2,1,0:T(4,128)S(1)}, f32[256,4,512]{2,1,0:T(4,128)}, u32[]{:S(2)}) copy-start(f32[256,4,512]{2,1,0:T(4,128)} %param.5) | copy-start | bytes 6291460

commit v2 on v1

--- a/solution.py
+++ b/solution.py
@@ -34,7 +34,7 @@
 
 
 def kernel(
-    g_hbm, m_hbm, back,
+    g_hbm, m_hbm, back, moved,
     gbuf, mbuf, D, R, X, G, GX, S, Z, QR, Y,
     gsem, msem, p1s, p1r, xs, xr, zs, zr, qs, qr, p2s, p2r, own1, own2,
 ):
@@ -53,17 +53,7 @@
     def dest(k):
         c, a, b = k // 16, (k % 16) // 4, k % 4
         z = side * a + (1 - side) * (3 - a)
-        return z * 8 + ((yy + 2 + b) % 4) * 2 + c
-
-    barrier = pltpu.get_barrier_semaphore()
-
-    @pl.loop(1, 32)
-    def _(k):
-        pl.semaphore_signal(barrier, inc=1, device_id=((s + k) % 32, m), device_id_type=MESH)
-
-    for k in range(1, 4):
-        pl.semaphore_signal(barrier, inc=1, device_id=(s, zh * 4 + (x + k) % 4), device_id_type=MESH)
-    pl.semaphore_signal(barrier, inc=1, device_id=partner, device_id_type=MESH)
+        return z * 8 + ((yy + 2 + b) % 4) * 2 + 1 - c
 
     pieces, size = 4, 1024
     loads = []
@@ -75,6 +65,17 @@
         ))
         loads[-1][0].start()
         loads[-1][1].start()
+
+    barrier = pltpu.get_barrier_semaphore()
+
+    @pl.loop(1, 32)
+    def _(k):
+        pl.semaphore_signal(barrier, inc=1, device_id=((s + k) % 32, m), device_id_type=MESH)
+
+    for k in range(1, 4):
+        pl.semaphore_signal(barrier, inc=1, device_id=(s, zh * 4 + (x + k) % 4), device_id_type=MESH)
+    pl.semaphore_signal(barrier, inc=1, device_id=partner, device_id_type=MESH)
+
     for i in range(pieces):
         loads[i][0].wait()
         loads[i][1].wait()
@@ -171,6 +172,11 @@
 
     def p2_own(r):
         return pltpu.make_async_copy(Y.at[r, s // 2, s % 2], p2_rows(mine, r), own2.at[r])
+
+    @pl.loop(0, 32)
+    def _(b):
+        rows = pl.ds(pl.multiple_of(b * 128, 128), 128)
+        moved[rows, :] = hold_rate * mbuf[rows, :] + gbuf[rows, :]
 
     for r in range(ROUNDS):
         @pl.loop(1, 32)
@@ -234,27 +240,31 @@
         p2_own(r).start()
 
     for r in range(ROUNDS):
+        p2_own(r).wait()
+        z_copy(r).wait_send()
+        for k in range(1, 4):
+            x_copy(r, (x + k) % 4, x).wait_send()
+            q_copy(r, (x + k) % 4, x).wait_send()
+
         @pl.loop(1, 32)
         def _(k):
             q = (s + k) % 32
-            p2_from(r, q).wait_recv()
             p1_copy(r, q).wait_send()
             p2_copy(r, q).wait_send()
 
-        p2_own(r).wait()
-        z_copy(r).wait_send()
-        for k in range(1, 4):
-            x_copy(r, (x + k) % 4, x).wait_send()
-            q_copy(r, (x + k) % 4, x).wait_send()
+    for r in range(ROUNDS):
+        @pl.loop(1, 32)
+        def _(k):
+            p2_from(r, (s + k) % 32).wait_recv()
 
 
 def exchange(g, m):
     dma = pltpu.SemaphoreType.DMA
     return pl.pallas_call(
         kernel,
-        out_shape=jax.ShapeDtypeStruct((4096, 128), F32),
-        in_specs=[pl.BlockSpec(memory_space=pl.ANY)] * 2,
-        out_specs=pl.BlockSpec(memory_space=pl.ANY),
+        out_shape=[jax.ShapeDtypeStruct((4096, 128), F32)] * 2,
+        in_specs=[pl.BlockSpec(memory_space=pltpu.HBM)] * 2,
+        out_specs=[pl.BlockSpec(memory_space=pltpu.VMEM)] * 2,
         scratch_shapes=[
             pltpu.VMEM((4096, 128), F32),
             pltpu.VMEM((4096, 128), F32),
@@ -282,6 +292,43 @@
     )(g, m)
 
 
+def finish_kernel(w, back, moved, new_w, new_m, held, wsem, msem):
+    momentum_out = pltpu.make_async_copy(moved, new_m, msem)
+    momentum_out.start()
+    pieces = 8
+    size = w.shape[0] // pieces
+    outs = []
+    for i in range(pieces):
+        part = pl.ds(i * size, size)
+
+        @pl.loop(0, size // 128)
+        def _(b):
+            rows = pl.ds(pl.multiple_of(i * size + b * 128, 128), 128)
+            held[rows, :] = w[rows, :] - learn_rate * back[rows, :]
+
+        outs.append(pltpu.make_async_copy(held.at[part], new_w.at[part], wsem.at[i]))
+        outs[-1].start()
+    for out in outs:
+        out.wait()
+    momentum_out.wait()
+
+
+def finish(w, back, moved):
+    return pl.pallas_call(
+        finish_kernel,
+        out_shape=[jax.ShapeDtypeStruct(w.shape, F32)] * 2,
+        in_specs=[pl.BlockSpec(memory_space=pltpu.VMEM)] * 3,
+        out_specs=[pl.BlockSpec(memory_space=pltpu.HBM)] * 2,
+        scratch_shapes=[
+            pltpu.VMEM(w.shape, F32),
+            pltpu.SemaphoreType.DMA((8,)),
+            pltpu.SemaphoreType.DMA(()),
+        ],
+        compiler_params=pltpu.CompilerParams(vmem_limit_bytes=16 * 1024 * 1024),
+        name="finish",
+    )(w, back, moved)
+
+
 def flat(a):
     return a.reshape(256, 4, 4, 128).transpose(0, 2, 1, 3).reshape(4096, 128)
 
@@ -292,9 +339,7 @@
 
 def local(gradients, momentum, weights):
     g, m, w = flat(gradients), flat(momentum), flat(weights)
-    back = exchange(g, m)
-    new_momentum = hold_rate * m + g
-    new_weights = w - learn_rate * back
+    new_weights, new_momentum = finish(w, *exchange(*(pltpu.with_memory_space_constraint(a, pltpu.HBM) for a in (g, m))))
     return (unflat(new_weights), unflat(new_momentum))
 
 

time: 113 us -> 106 us (0.938)
  the two profiles are of different devices: /device:TPU:1 before, /device:TPU:32 now
where the time goes in v2:
time: 106 us
  Pallas kernels  105 us (99%)
    pallas_call x1, Pallas kernels, exchange(): pl.pallas_call(kernel, out_shape=[jax.ShapeDtypeStruct((4096, 128), F32)]...  103 us

profile of v2, /device:TPU:32, one launch (start us, length us, event | category | flops | bytes accessed | tf_op | source)
XLA Modules:
  0.0 105.8 jit_solution(16988259820564473702)
XLA Ops:
  0.6 0.0 copy-start
  0.6 103.1 %exchange.1 = (f32[4096,128]{1,0:T(8,128)S(1)}, f32[4096,128]{1,0:T(8,128)S(1)}) custom-call(f32[4096,128]{1,0:T(8,128)} %bitcast.26, f32[4096,128]{1,0:T(8,128)} %bitcast.27), custom_call_target="tpu_custom_call" | custom-call | tf_op jit(solution)/shard_map/exchange/pallas_call | solution.py:263
  103.7 0.0 copy-done
  103.7 2.1 %finish.1 = (f32[4096,128]{1,0:T(8,128)}, f32[4096,128]{1,0:T(8,128)}) custom-call(f32[4096,128]{1,0:T(8,128)S(1)} %bitcast.25, f32[4096,128]{1,0:T(8,128)S(1)} %get-tuple-element.6.back, f32[4096,128]{1,0:T(8,128)S(1)} %get-tuple-element.7.moved), custom_call_target="tpu_custom_call" | custom-call | tf_op jit(solution)/shard_map/finish/pallas_call | solution.py:317
Async XLA Ops:
  0.6 103.1 %copy-start = (f32[256,4,512]{2,1,0:T(4,128)S(1)}, f32[256,4,512]{2,1,0:T(4,128)}, u32[]{:S(2)}) copy-start(f32[256,4,512]{2,1,0:T(4,128)} %param.5) | copy-start | bytes 6291460

commit v3 on v0

v3 whole, which is shorter than its diff:
```python
import contextlib

import jax
import jax.numpy as jnp
from jax import lax
from jax.experimental import pallas as pl
from jax.experimental.pallas import tpu as pltpu
from jax.sharding import PartitionSpec as P

MESH = pl.DeviceIdType.MESH
F32 = jnp.float32
ITERS = 4
ROUNDS = 2
PER = 4
BLOCKS = (16, 2, ROUNDS, 64, 128)
hold_rate = 0.9
learn_rate = 0.8
HI = lax.Precision.HIGHEST


def scope(name):
    return contextlib.nullcontext()


def dot(a, b):
    return lax.dot_general(a, b, (((1,), (0,)), ((), ())), precision=HI, preferred_element_type=F32)


def dot_t(a, b):
    return lax.dot_general(a, b, (((1,), (1,)), ((), ())), precision=HI, preferred_element_type=F32)


def merge_halves(a, b):
    low = lax.broadcasted_iota(jnp.int32, a.shape, 1) < 4
    return (
        jnp.where(low, a, pltpu.roll(b, 4, 1)),
        jnp.where(low, pltpu.roll(a, 4, 1), b),
    )


def remote(src, dst, send, recv, to):
    return pltpu.make_async_remote_copy(
        src_ref=src, dst_ref=dst, send_sem=send, recv_sem=recv, device_id=to, device_id_type=MESH
    )


def wait_bytes(ref, sem):
    pltpu.make_async_copy(ref, ref, sem).wait()


def kernel(
    g_hbm, m_hbm, back, moved,
    gbuf, mbuf, D, R, X, G, GX, S, Z, QR, Y,
    gsem, msem, p1s, p1r, xs, xr, zs, zr, qs, qr, p2s, p2r, ready,
):
    s, m = lax.axis_index("shard"), lax.axis_index("model")
    zl, yy, core = s // 8, (s // 2) % 4, s % 2
    zh, x = m // 4, m % 4
    side = zl // 2

    loads = []
    for q in range(4):
        c, r = 1 - q % 2, q // 2
        loads.append((
            pltpu.make_async_copy(g_hbm.at[:, c, r], gbuf.at[q], gsem.at[q]),
            pltpu.make_async_copy(m_hbm.at[:, c, r], mbuf.at[q], msem.at[q]),
        ))
        loads[-1][0].start()
        loads[-1][1].start()

    def group_of(d):
        z = d // 8
        return (zh * (3 - z) + (1 - zh) * z) * 8 + d % 8

    mine = group_of(s)
    partner = ((3 - zl) * 8 + s % 8, (1 - zh) * 4 + x)

    def dest(c, k):
        a, b = k // 4, k % 4
        z = side * a + (1 - side) * (3 - a)
        return z * 8 + ((yy + 2 + b) % 4) * 2 + c

    barrier = pltpu.get_barrier_semaphore()

    @pl.when(zh == 0)
    def _():
        pl.semaphore_signal(barrier, inc=1, device_id=partner, device_id_type=MESH)

    @pl.loop(1, 32)
    def _(k):
        pl.semaphore_signal(barrier, inc=1, device_id=((s + k) % 32, m), device_id_type=MESH)

    for k in range(1, 4):
        pl.semaphore_signal(barrier, inc=1, device_id=(s, zh * 4 + (x + k) % 4), device_id_type=MESH)

    for q in range(4):
        c, r = 1 - q % 2, q // 2
        with scope(f"load#q={q}"):
            loads[q][0].wait()
            loads[q][1].wait()

            @pl.loop(0, 8)
            def _(b):
                both = pl.ds(b * 2, 2)
                g = gbuf[q, both]
                D[q, both] = hold_rate * (hold_rate * mbuf[q, both] + g) + g

        if q == 0:
            with scope("barrier"):
                pl.semaphore_wait(barrier, 34 + zh)

            @pl.when(zh == 1)
            def _():
                pl.semaphore_signal(ready, inc=1, device_id=partner, device_id_type=MESH)

        with scope(f"p1send#q={q}"):
            @pl.loop(0, 16)
            def _(k):
                d = dest(c, k)
                rows = D.at[q, group_of(d) // 2]
                place = R.at[r, s // 2, s % 2]

                @pl.when(d != s)
                def _():
                    remote(rows, place, p1s.at[r], p1r.at[r], (d, m)).start()

                @pl.when(d == s)
                def _():
                    pltpu.make_async_copy(rows, place, p1r.at[r]).start()

    with scope("moved"):
        for q in range(4):
            c, r = 1 - q % 2, q // 2

            @pl.loop(0, 8)
            def _(b):
                both = pl.ds(b * 2, 2)
                moved[both, c, r] = hold_rate * mbuf[q, both] + gbuf[q, both]

    eye = (
        lax.broadcasted_iota(jnp.int32, (128, 128), 0) == lax.broadcasted_iota(jnp.int32, (128, 128), 1)
    ).astype(F32)

    for r in range(ROUNDS):
        with scope(f"p1wait#r={r}"):
            wait_bytes(R.at[r], p1r.at[r])

        with scope(f"gram#r={r}"):
            @pl.loop(0, PER)
            def _(j):
                for h in range(2):
                    rows = pl.ds(pl.multiple_of(j * 16 + h * 8, 8), 8)
                    low, high = merge_halves(R[r, :, 0, rows, :], R[r, :, 1, rows, :])
                    X[j, :, 256 * h : 256 * h + 128] = low.reshape(128, 128)
                    X[j, :, 256 * h + 128 : 256 * h + 256] = high.reshape(128, 128)
                G[r, j] = dot_t(X[j], X[j])

        with scope(f"xred#r={r}"):
            for k in range(1, 4):
                q = (x + k) % 4
                remote(G.at[r, q], GX.at[r, 3 - k], xs.at[r], xr.at[r], (s, zh * 4 + q)).start()
            wait_bytes(GX.at[r], xr.at[r])
            S[r] = G[r, x] + GX[r, 0] + GX[r, 1] + GX[r, 2]

        with scope(f"zred#r={r}"):
            if r == 0:
                @pl.when(zh == 0)
                def _():
                    pl.semaphore_wait(ready, 1)

            across = remote(S.at[r], Z.at[r], zs.at[r], zr.at[r], partner)
            across.start()
            across.wait_recv()

        with scope(f"chain#r={r}"):
            gram = S[r] + Z[r]
            scale = lax.rsqrt(jnp.sum(jnp.sum(gram * eye, axis=1, keepdims=True), axis=0, keepdims=True) + 1e-06)
            gram = gram * (scale * scale)
            factor = None
            for step in range(ITERS):
                mixed = 3.4445 * eye + (-4.775 * gram + 2.0315 * dot(gram, gram))
                factor = mixed if factor is None else dot(mixed, factor)
                if step < ITERS - 1:
                    gram = dot(dot(mixed, gram), mixed)
            QR[r, x] = factor * scale

        with scope(f"qcast#r={r}"):
            for k in range(1, 4):
                to = (s, zh * 4 + (x + k) % 4)
                remote(QR.at[r, x], QR.at[r, x], qs.at[r], qr.at[r], to).start()
            wait_bytes(GX.at[r], qr.at[r])

        with scope(f"apply#r={r}"):
            @pl.loop(0, PER)
            def _(j):
                for h in range(2):
                    wide = dot(QR[r, j], X[j, :, 256 * h : 256 * h + 256])
                    rows = pl.ds(pl.multiple_of(j * 16 + h * 8, 8), 8)
                    even, odd = merge_halves(wide[:, :128].reshape(16, 8, 128), wide[:, 128:].reshape(16, 8, 128))
                    Y[r, :, 0, rows, :] = even
                    Y[r, :, 1, rows, :] = odd

        with scope(f"p2send#r={r}"):
            for c in (1, 0):
                @pl.loop(0, 16)
                def _(k):
                    d = dest(c, k)
                    rows = Y.at[r, d // 2, c]
                    place = back.at[mine // 2, mine % 2, r]

                    @pl.when(d != s)
                    def _():
                        remote(rows, place, p2s.at[r], p2r.at[r], (d, m)).start()

                    @pl.when(d == s)
                    def _():
                        pltpu.make_async_copy(rows, place, p2r.at[r]).start()

    with scope("sendwait"):
        for r in range(ROUNDS):
            three = GX.at[r]
            wait_bytes(three, xs.at[r])
            wait_bytes(three, qs.at[r])
            wait_bytes(S.at[r], zs.at[r])
            for sem in (p1s, p2s):
                wait_bytes(Y.at[r, pl.ds(0, 15)], sem.at[r])
                wait_bytes(Y.at[r, 15, 0], sem.at[r])

    for r in range(ROUNDS):
        with scope(f"p2wait#r={r}"):
            wait_bytes(R.at[r], p2r.at[r])


def exchange(g, m):
    dma = pltpu.SemaphoreType.DMA
    quarters = pltpu.VMEM((4, 16, 64, 128), F32)
    moving = pltpu.VMEM((ROUNDS, 16, 2, 64, 128), F32)
    square = (128, 128)
    return pl.pallas_call(
        kernel,
        out_shape=[jax.ShapeDtypeStruct(BLOCKS, F32)] * 2,
        in_specs=[pl.BlockSpec(memory_space=pltpu.HBM)] * 2,
        out_specs=[pl.BlockSpec(memory_space=pltpu.VMEM)] * 2,
        scratch_shapes=[
            quarters, quarters, quarters,
            moving,
            pltpu.VMEM((PER, 128, 512), F32),
            pltpu.VMEM((ROUNDS, PER, *square), F32),
            pltpu.VMEM((ROUNDS, 3, *square), F32),
            pltpu.VMEM((ROUNDS, *square), F32),
            pltpu.VMEM((ROUNDS, *square), F32),
            pltpu.VMEM((ROUNDS, PER, *square), F32),
            moving,
            dma((4,)), dma((4,)),
            *[dma((ROUNDS,))] * 10,
            pltpu.SemaphoreType.REGULAR,
        ],
        compiler_params=pltpu.CompilerParams(
            collective_id=0, has_side_effects=True, vmem_limit_bytes=40 * 1024 * 1024
        ),
        name="exchange",
    )(g, m)


def finish_kernel(w, back, moved, new_w, new_m, held, wsem, msem):
    momentum_out = pltpu.make_async_copy(moved, new_m, msem)
    momentum_out.start()
    pieces = 8
    size = w.shape[0] // pieces
    outs = []
    for i in range(pieces):
        part = pl.ds(i * size, size)

        @pl.loop(0, size // 128)
        def _(b):
            rows = pl.ds(pl.multiple_of(i * size + b * 128, 128), 128)
            held[rows, :] = w[rows, :] - learn_rate * back[rows, :]

        outs.append(pltpu.make_async_copy(held.at[part], new_w.at[part], wsem.at[i]))
        outs[-1].start()
    for out in outs:
        out.wait()
    momentum_out.wait()


def finish(w, back, moved):
    return pl.pallas_call(
        finish_kernel,
        out_shape=[jax.ShapeDtypeStruct(w.shape, F32)] * 2,
        in_specs=[pl.BlockSpec(memory_space=pltpu.VMEM)] * 3,
        out_specs=[pl.BlockSpec(memory_space=pltpu.HBM)] * 2,
        scratch_shapes=[
            pltpu.VMEM(w.shape, F32),
            pltpu.SemaphoreType.DMA((8,)),
            pltpu.SemaphoreType.DMA(()),
        ],
        compiler_params=pltpu.CompilerParams(vmem_limit_bytes=16 * 1024 * 1024),
        name="finish",
    )(w, back, moved)


def flat(a):
    return a.reshape(256, 4, 4, 128).transpose(0, 2, 1, 3).reshape(4096, 128)


def unflat(a):
    return a.reshape(256, 4, 4, 128).transpose(0, 2, 1, 3).reshape(256, 4, 512)


def local(gradients, momentum, weights):
    g, m, w = flat(gradients), flat(momentum), flat(weights)
    inputs = [pltpu.with_memory_space_constraint(a.reshape(BLOCKS), pltpu.HBM) for a in (g, m)]
    back, moved = (a.reshape(4096, 128) for a in exchange(*inputs))
    new_weights, new_momentum = finish(w, back, moved)
    return (unflat(new_weights), unflat(new_momentum))


def solution(mesh):
    placed = P(None, "shard", "model")
    return jax.shard_map(
        local, mesh=mesh, in_specs=(placed,) * 3, out_specs=(placed, placed), check_vma=False
    )
```

time: 272 us -> 103 us (0.38); the launches traced: 269 us -> 103 us
  blocking collectives: 167 us -> 0 us
  Pallas kernels: 0 us -> 102 us
  waiting for transfers between devices: 42.1 us -> 0 us
  local copies, waits for them, and re-layouts: 25.6 us -> 0.01 us
  matrix products: 17.9 us -> 0 us
  other arithmetic: 9.74 us -> 0 us
  starting transfers between devices: 5.06 us -> 0 us
    all_to_all x4 -> x0, blocking collectives: 167 us -> none  [the longest x2 62.7 us: turned_blocks(): filled = lax.all_to_all(filled, axes[k], k, k, tiled=True)]
    pallas_call x0 -> x2, Pallas kernels: none -> 102 us  [the longest x1 100 us: exchange(): pl.pallas_call(kernel, out_shape=[jax.ShapeDtypeStruct(BLOCKS, F32)] * 2,...]
    all_to_all x1 -> x0, waiting for transfers between devices: 42.1 us -> none  [local(): lax.all_to_all(iterate, SHARD, split_axis=1, concat_axis=0, tiled=True)]
    dot_general x12 -> x0, matrix products: 17.9 us -> none  [the longest x4 9.94 us: local(): jnp.einsum('mij,mjk->mik', mixed, iterate, precision=lax.Precision.HIGHEST)]
    unnamed x4 -> x2, local copies, waits for them, and re-layouts: 8.27 us -> 0.01 us
    mul x3 -> x0, local copies, waits for them, and re-layouts: 7.7 us -> none  [the longest x2 5.8 us: local(): 3.4445 * iterate]
    all_to_all x1 -> x0, starting transfers between devices: 5.06 us -> none  [local(): lax.all_to_all(iterate, SHARD, split_axis=1, concat_axis=0, tiled=True)]
    add x1 -> x0, other arithmetic: 4.89 us -> none  [local(): new_momentum = hold_rate * momentum + gradients]
  transfers between devices with their start and end apart: 1 -> 0, of which waited for: 1 -> 0; matrix products, arithmetic and copies ran while one was open for 2% -> 0% of each run, Pallas kernels for 0% -> 0%
where the time goes in v3:
time: 103 us
  Pallas kernels  102 us (99%)
    pallas_call x1, Pallas kernels, exchange(): pl.pallas_call(kernel, out_shape=[jax.ShapeDtypeStruct(BLOCKS, F32)] * 2,...  100 us
    pallas_call x1, Pallas kernels, finish(): pl.pallas_call(finish_kernel, out_shape=[jax.ShapeDtypeStruct(w.shape, F3...  2.08 us

profile of v3, /device:TPU:32, one launch (start us, length us, event | category | flops | bytes accessed | tf_op | source)
XLA Modules:
  0.0 102.8 jit_solution(17102916394111907488)
XLA Ops:
  0.6 0.0 copy-start
  0.6 100.1 %exchange.1 = (f32[16,2,2,64,128]{4,3,2,1,0:T(8,128)S(1)}, f32[16,2,2,64,128]{4,3,2,1,0:T(8,128)S(1)}) custom-call(f32[16,2,2,64,128]{4,3,2,1,0:T(8,128)} %bitcast.30, f32[16,2,2,64,128]{4,3,2,1,0:T(8,128)} %bitcast.31), custom_call_target="tpu_custom_call" | custom-call | tf_op jit(solution)/shard_map/exchange/pallas_call | solution.py:239
  100.7 0.0 copy-done
  100.8 2.1 %finish.1 = (f32[4096,128]{1,0:T(8,128)}, f32[4096,128]{1,0:T(8,128)}) custom-call(f32[4096,128]{1,0:T(8,128)S(1)} %bitcast.27, f32[4096,128]{1,0:T(8,128)S(1)} %bitcast.28, f32[4096,128]{1,0:T(8,128)S(1)} %bitcast.29), custom_call_target="tpu_custom_call" | custom-call | tf_op jit(solution)/shard_map/finish/pallas_call | solution.py:287
Async XLA Ops:
  0.6 100.1 %copy-start = (f32[256,4,512]{2,1,0:T(4,128)S(1)}, f32[256,4,512]{2,1,0:T(4,128)}, u32[]{:S(2)}) copy-start(f32[256,4,512]{2,1,0:T(4,128)} %param.5) | copy-start | bytes 6291460

commit v4 on v3

--- a/solution.py
+++ b/solution.py
@@ -58,6 +58,32 @@
     zh, x = m // 4, m % 4
     side = zl // 2
 
+    def group_of(d):
+        z = d // 8
+        return (zh * (3 - z) + (1 - zh) * z) * 8 + d % 8
+
+    mine = group_of(s)
+    partner = ((3 - zl) * 8 + s % 8, (1 - zh) * 4 + x)
+
+    def dest(c, k):
+        a, b = k // 4, k % 4
+        z = side * a + (1 - side) * (3 - a)
+        return z * 8 + ((yy + 2 + b) % 4) * 2 + c
+
+    barrier = pltpu.get_barrier_semaphore()
+
+    @pl.when(zh == 0)
+    def _():
+        pl.semaphore_signal(barrier, inc=1, device_id=partner, device_id_type=MESH)
+
+    for k in (16, 24, 8):
+        for i in range(8):
+            pl.semaphore_signal(barrier, inc=1, device_id=((s + k + i) % 32, m), device_id_type=MESH)
+    for k in range(1, 8):
+        pl.semaphore_signal(barrier, inc=1, device_id=((s + k) % 32, m), device_id_type=MESH)
+    for k in range(1, 4):
+        pl.semaphore_signal(barrier, inc=1, device_id=(s, zh * 4 + (x + k) % 4), device_id_type=MESH)
+
     loads = []
     for q in range(4):
         c, r = 1 - q % 2, q // 2
@@ -68,30 +94,6 @@
         loads[-1][0].start()
         loads[-1][1].start()
 
-    def group_of(d):
-        z = d // 8
-        return (zh * (3 - z) + (1 - zh) * z) * 8 + d % 8
-
-    mine = group_of(s)
-    partner = ((3 - zl) * 8 + s % 8, (1 - zh) * 4 + x)
-
-    def dest(c, k):
-        a, b = k // 4, k % 4
-        z = side * a + (1 - side) * (3 - a)
-        return z * 8 + ((yy + 2 + b) % 4) * 2 + c
-
-    barrier = pltpu.get_barrier_semaphore()
-
-    @pl.when(zh == 0)
-    def _():
-        pl.semaphore_signal(barrier, inc=1, device_id=partner, device_id_type=MESH)
-
-    @pl.loop(1, 32)
-    def _(k):
-        pl.semaphore_signal(barrier, inc=1, device_id=((s + k) % 32, m), device_id_type=MESH)
-
-    for k in range(1, 4):
-        pl.semaphore_signal(barrier, inc=1, device_id=(s, zh * 4 + (x + k) % 4), device_id_type=MESH)
 
     for q in range(4):
         c, r = 1 - q % 2, q // 2
@@ -141,7 +143,7 @@
         lax.broadcasted_iota(jnp.int32, (128, 128), 0) == lax.broadcasted_iota(jnp.int32, (128, 128), 1)
     ).astype(F32)
 
-    for r in range(ROUNDS):
+    def gram_step(r):
         with scope(f"p1wait#r={r}"):
             wait_bytes(R.at[r], p1r.at[r])
 
@@ -151,26 +153,28 @@
                 for h in range(2):
                     rows = pl.ds(pl.multiple_of(j * 16 + h * 8, 8), 8)
                     low, high = merge_halves(R[r, :, 0, rows, :], R[r, :, 1, rows, :])
-                    X[j, :, 256 * h : 256 * h + 128] = low.reshape(128, 128)
-                    X[j, :, 256 * h + 128 : 256 * h + 256] = high.reshape(128, 128)
-                G[r, j] = dot_t(X[j], X[j])
-
-        with scope(f"xred#r={r}"):
+                    X[r, j, :, 256 * h : 256 * h + 128] = low.reshape(128, 128)
+                    X[r, j, :, 256 * h + 128 : 256 * h + 256] = high.reshape(128, 128)
+                G[r, j] = dot_t(X[r, j], X[r, j])
+
             for k in range(1, 4):
                 q = (x + k) % 4
                 remote(G.at[r, q], GX.at[r, 3 - k], xs.at[r], xr.at[r], (s, zh * 4 + q)).start()
+
+    def sum_step(r):
+        with scope(f"xred#r={r}"):
             wait_bytes(GX.at[r], xr.at[r])
             S[r] = G[r, x] + GX[r, 0] + GX[r, 1] + GX[r, 2]
-
-        with scope(f"zred#r={r}"):
             if r == 0:
                 @pl.when(zh == 0)
                 def _():
                     pl.semaphore_wait(ready, 1)
 
-            across = remote(S.at[r], Z.at[r], zs.at[r], zr.at[r], partner)
-            across.start()
-            across.wait_recv()
+            remote(S.at[r], Z.at[r], zs.at[r], zr.at[r], partner).start()
+
+    def chain_step(r):
+        with scope(f"zred#r={r}"):
+            remote(S.at[r], Z.at[r], zs.at[r], zr.at[r], partner).wait_recv()
 
         with scope(f"chain#r={r}"):
             gram = S[r] + Z[r]
@@ -183,18 +187,19 @@
                 if step < ITERS - 1:
                     gram = dot(dot(mixed, gram), mixed)
             QR[r, x] = factor * scale
-
-        with scope(f"qcast#r={r}"):
             for k in range(1, 4):
                 to = (s, zh * 4 + (x + k) % 4)
                 remote(QR.at[r, x], QR.at[r, x], qs.at[r], qr.at[r], to).start()
+
+    def apply_step(r):
+        with scope(f"qcast#r={r}"):
             wait_bytes(GX.at[r], qr.at[r])
 
         with scope(f"apply#r={r}"):
             @pl.loop(0, PER)
             def _(j):
                 for h in range(2):
-                    wide = dot(QR[r, j], X[j, :, 256 * h : 256 * h + 256])
+                    wide = dot(QR[r, j], X[r, j, :, 256 * h : 256 * h + 256])
                     rows = pl.ds(pl.multiple_of(j * 16 + h * 8, 8), 8)
                     even, odd = merge_halves(wide[:, :128].reshape(16, 8, 128), wide[:, 128:].reshape(16, 8, 128))
                     Y[r, :, 0, rows, :] = even
@@ -216,6 +221,23 @@
                     def _():
                         pltpu.make_async_copy(rows, place, p2r.at[r]).start()
 
+    gram_step(0)
+    sum_step(0)
+    chain_step(0)
+
+    @pl.when(zh == 1)
+    def _():
+        gram_step(1)
+
+    apply_step(0)
+
+    @pl.when(jnp.logical_not(zh == 1))
+    def _():
+        gram_step(1)
+
+    sum_step(1)
+    chain_step(1)
+    apply_step(1)
     with scope("sendwait"):
         for r in range(ROUNDS):
             three = GX.at[r]
@@ -244,7 +266,7 @@
         scratch_shapes=[
             quarters, quarters, quarters,
             moving,
-            pltpu.VMEM((PER, 128, 512), F32),
+            pltpu.VMEM((ROUNDS, PER, 128, 512), F32),
             pltpu.VMEM((ROUNDS, PER, *square), F32),
             pltpu.VMEM((ROUNDS, 3, *square), F32),
             pltpu.VMEM((ROUNDS, *square), F32),

time: 103 us -> 102 us (level)
    pallas_call x1, Pallas kernels: 100 us -> 98.6 us  [exchange(): pl.pallas_call(kernel, out_shape=[jax.ShapeDtypeStruct(BLOCKS, F32)] * 2,...]
where the time goes in v4:
time: 102 us; the launch traced here: 101 us
  Pallas kernels  101 us (99%)
    pallas_call x1, Pallas kernels, exchange(): pl.pallas_call(kernel, out_shape=[jax.ShapeDtypeStruct(BLOCKS, F32)] * 2,...  98.6 us
    pallas_call x1, Pallas kernels, finish(): pl.pallas_call(finish_kernel, out_shape=[jax.ShapeDtypeStruct(w.shape, F3...  2.08 us

profile of v4, /device:TPU:32, one launch (start us, length us, event | category | flops | bytes accessed | tf_op | source)
XLA Modules:
  0.0 101.3 jit_solution(12339729734294780688)
XLA Ops:
  0.6 0.0 copy-start
  0.6 98.6 %exchange.1 = (f32[16,2,2,64,128]{4,3,2,1,0:T(8,128)S(1)}, f32[16,2,2,64,128]{4,3,2,1,0:T(8,128)S(1)}) custom-call(f32[16,2,2,64,128]{4,3,2,1,0:T(8,128)} %bitcast.30, f32[16,2,2,64,128]{4,3,2,1,0:T(8,128)} %bitcast.31), custom_call_target="tpu_custom_call" | custom-call | tf_op jit(solution)/shard_map/exchange/pallas_call | solution.py:261
  99.2 0.0 copy-done
  99.3 2.1 %finish.1 = (f32[4096,128]{1,0:T(8,128)}, f32[4096,128]{1,0:T(8,128)}) custom-call(f32[4096,128]{1,0:T(8,128)S(1)} %bitcast.27, f32[4096,128]{1,0:T(8,128)S(1)} %bitcast.28, f32[4096,128]{1,0:T(8,128)S(1)} %bitcast.29), custom_call_target="tpu_custom_call" | custom-call | tf_op jit(solution)/shard_map/finish/pallas_call | solution.py:309
Async XLA Ops:
  0.6 98.6 %copy-start = (f32[256,4,512]{2,1,0:T(4,128)S(1)}, f32[256,4,512]{2,1,0:T(4,128)}, u32[]{:S(2)}) copy-start(f32[256,4,512]{2,1,0:T(4,128)} %param.5) | copy-start | bytes 6291460

commit v5 on v4

--- a/solution.py
+++ b/solution.py
@@ -49,15 +49,29 @@
 
 
 def kernel(
-    g_hbm, m_hbm, back, moved,
+    g_hbm, m_hbm, w_hbm, back, moved, held_w,
     gbuf, mbuf, D, R, X, G, GX, S, Z, QR, Y,
-    gsem, msem, p1s, p1r, xs, xr, zs, zr, qs, qr, p2s, p2r, ready,
+    wsem, gsem, msem, p1s, p1r, xs, xr, zs, zr, qs, qr, p2s, p2r, ready,
 ):
     s, m = lax.axis_index("shard"), lax.axis_index("model")
     zl, yy, core = s // 8, (s // 2) % 4, s % 2
     zh, x = m // 4, m % 4
     side = zl // 2
 
+    loads = []
+    for q in range(4):
+        c, r = 1 - q % 2, q // 2
+        loads.append((
+            pltpu.make_async_copy(g_hbm.at[:, c, r], gbuf.at[q], gsem.at[q]),
+            pltpu.make_async_copy(m_hbm.at[:, c, r], mbuf.at[q], msem.at[q]),
+        ))
+
+    def load(q):
+        for copy in loads[q]:
+            copy.start()
+
+    load(0)
+
     def group_of(d):
         z = d // 8
         return (zh * (3 - z) + (1 - zh) * z) * 8 + d % 8
@@ -69,6 +83,11 @@
         a, b = k // 4, k % 4
         z = side * a + (1 - side) * (3 - a)
         return z * 8 + ((yy + 2 + b) % 4) * 2 + c
+
+    def late_dest(c, k):
+        half, a, b = k // 8, (k % 8) // 2, k % 2
+        z = side * a + (1 - side) * (3 - a)
+        return z * 8 + (half * 2 + (yy + 1 + b) % 2) * 2 + c
 
     barrier = pltpu.get_barrier_semaphore()
 
@@ -84,22 +103,15 @@
     for k in range(1, 4):
         pl.semaphore_signal(barrier, inc=1, device_id=(s, zh * 4 + (x + k) % 4), device_id_type=MESH)
 
-    loads = []
-    for q in range(4):
-        c, r = 1 - q % 2, q // 2
-        loads.append((
-            pltpu.make_async_copy(g_hbm.at[:, c, r], gbuf.at[q], gsem.at[q]),
-            pltpu.make_async_copy(m_hbm.at[:, c, r], mbuf.at[q], msem.at[q]),
-        ))
-        loads[-1][0].start()
-        loads[-1][1].start()
-
 
     for q in range(4):
         c, r = 1 - q % 2, q // 2
         with scope(f"load#q={q}"):
-            loads[q][0].wait()
-            loads[q][1].wait()
+            for copy in loads[q]:
+                copy.wait()
+            if q == 0:
+                for later in range(1, 4):
+                    load(later)
 
             @pl.loop(0, 8)
             def _(b):
@@ -129,6 +141,8 @@
                 @pl.when(d == s)
                 def _():
                     pltpu.make_async_copy(rows, place, p1r.at[r]).start()
+
+    pltpu.make_async_copy(w_hbm, held_w, wsem).start()
 
     with scope("moved"):
         for q in range(4):
@@ -209,7 +223,7 @@
             for c in (1, 0):
                 @pl.loop(0, 16)
                 def _(k):
-                    d = dest(c, k)
+                    d = late_dest(c, k) if c in (0, 1) else dest(c, k)
                     rows = Y.at[r, d // 2, c]
                     place = back.at[mine // 2, mine % 2, r]
 
@@ -239,6 +253,7 @@
     chain_step(1)
     apply_step(1)
     with scope("sendwait"):
+        pltpu.make_async_copy(w_hbm, held_w, wsem).wait()
         for r in range(ROUNDS):
             three = GX.at[r]
             wait_bytes(three, xs.at[r])
@@ -253,16 +268,16 @@
             wait_bytes(R.at[r], p2r.at[r])
 
 
-def exchange(g, m):
+def exchange(g, m, w):
     dma = pltpu.SemaphoreType.DMA
     quarters = pltpu.VMEM((4, 16, 64, 128), F32)
     moving = pltpu.VMEM((ROUNDS, 16, 2, 64, 128), F32)
     square = (128, 128)
     return pl.pallas_call(
         kernel,
-        out_shape=[jax.ShapeDtypeStruct(BLOCKS, F32)] * 2,
-        in_specs=[pl.BlockSpec(memory_space=pltpu.HBM)] * 2,
-        out_specs=[pl.BlockSpec(memory_space=pltpu.VMEM)] * 2,
+        out_shape=[jax.ShapeDtypeStruct(BLOCKS, F32)] * 3,
+        in_specs=[pl.BlockSpec(memory_space=pltpu.HBM)] * 3,
+        out_specs=[pl.BlockSpec(memory_space=pltpu.VMEM)] * 3,
         scratch_shapes=[
             quarters, quarters, quarters,
             moving,
@@ -273,7 +288,7 @@
             pltpu.VMEM((ROUNDS, *square), F32),
             pltpu.VMEM((ROUNDS, PER, *square), F32),
             moving,
-            dma((4,)), dma((4,)),
+            dma(()), dma((4,)), dma((4,)),
             *[dma((ROUNDS,))] * 10,
             pltpu.SemaphoreType.REGULAR,
         ],
@@ -281,7 +296,7 @@
             collective_id=0, has_side_effects=True, vmem_limit_bytes=40 * 1024 * 1024
         ),
         name="exchange",
-    )(g, m)
+    )(g, m, w)
 
 
 def finish_kernel(w, back, moved, new_w, new_m, held, wsem, msem):
@@ -331,8 +346,8 @@
 
 def local(gradients, momentum, weights):
     g, m, w = flat(gradients), flat(momentum), flat(weights)
-    inputs = [pltpu.with_memory_space_constraint(a.reshape(BLOCKS), pltpu.HBM) for a in (g, m)]
-    back, moved = (a.reshape(4096, 128) for a in exchange(*inputs))
+    inputs = [pltpu.with_memory_space_constraint(a.reshape(BLOCKS), pltpu.HBM) for a in (g, m, w)]
+    back, moved, w = (a.reshape(4096, 128) for a in exchange(*inputs))
     new_weights, new_momentum = finish(w, back, moved)
     return (unflat(new_weights), unflat(new_momentum))
 

time: 102 us -> 101 us (level)
  Pallas kernels: 101 us -> 99.4 us
    pallas_call x1, Pallas kernels: 98.6 us -> 97.3 us  [exchange(): pl.pallas_call(kernel, out_shape=[jax.ShapeDtypeStruct(BLOCKS, F32)] * 3,...]
where the time goes in v5:
time: 101 us; the launch traced here: 100 us
  Pallas kernels  99.4 us (98%)
    pallas_call x1, Pallas kernels, exchange(): pl.pallas_call(kernel, out_shape=[jax.ShapeDtypeStruct(BLOCKS, F32)] * 3,...  97.3 us
    pallas_call x1, Pallas kernels, finish(): pl.pallas_call(finish_kernel, out_shape=[jax.ShapeDtypeStruct(w.shape, F3...  2.08 us

profile of v5, /device:TPU:32, one launch (start us, length us, event | category | flops | bytes accessed | tf_op | source)
XLA Modules:
  0.0 100.1 jit_solution(9459472386284948172)
XLA Ops:
  0.6 97.3 %exchange.1 = (f32[16,2,2,64,128]{4,3,2,1,0:T(8,128)S(1)}, f32[16,2,2,64,128]{4,3,2,1,0:T(8,128)S(1)}, f32[16,2,2,64,128]{4,3,2,1,0:T(8,128)S(1)}) custom-call(f32[16,2,2,64,128]{4,3,2,1,0:T(8,128)} %bitcast.31, f32[16,2,2,64,128]{4,3,2,1,0:T(8,128)} %bitcast.32, f32[16,2,2,64,128]{4,3,2,1,0:T(8,128)} %bitcast.33), custom_call_target="tpu_custom_call" | custom-call | tf_op jit(solution)/shard_map/exchange/pallas_call | solution.py:276
  98.0 2.1 %finish.1 = (f32[4096,128]{1,0:T(8,128)}, f32[4096,128]{1,0:T(8,128)}) custom-call(f32[4096,128]{1,0:T(8,128)S(1)} %bitcast.30, f32[4096,128]{1,0:T(8,128)S(1)} %bitcast.28, f32[4096,128]{1,0:T(8,128)S(1)} %bitcast.29), custom_call_target="tpu_custom_call" | custom-call | tf_op jit(solution)/shard_map/finish/pallas_call | solution.py:324

commit v6 on v5

--- a/solution.py
+++ b/solution.py
@@ -10,6 +10,7 @@
 MESH = pl.DeviceIdType.MESH
 F32 = jnp.float32
 ITERS = 4
+LINEAR = 3.4445
 ROUNDS = 2
 PER = 4
 BLOCKS = (16, 2, ROUNDS, 64, 128)
@@ -194,13 +195,15 @@
             gram = S[r] + Z[r]
             scale = lax.rsqrt(jnp.sum(jnp.sum(gram * eye, axis=1, keepdims=True), axis=0, keepdims=True) + 1e-06)
             gram = gram * (scale * scale)
-            factor = None
+            n = []
             for step in range(ITERS):
-                mixed = 3.4445 * eye + (-4.775 * gram + 2.0315 * dot(gram, gram))
-                factor = mixed if factor is None else dot(mixed, factor)
+                n.append(-4.775 * gram + 2.0315 * dot(gram, gram))
                 if step < ITERS - 1:
+                    mixed = LINEAR * eye + n[-1]
                     gram = dot(dot(mixed, gram), mixed)
-            QR[r, x] = factor * scale
+            early = LINEAR * (n[0] + n[1]) + dot(n[1], n[0])
+            late = LINEAR * (n[2] + n[3]) + dot(n[3], n[2])
+            QR[r, x] = (LINEAR**4 * eye + (LINEAR**2 * (early + late) + dot(late, early))) * scale
             for k in range(1, 4):
                 to = (s, zh * 4 + (x + k) % 4)
                 remote(QR.at[r, x], QR.at[r, x], qs.at[r], qr.at[r], to).start()

time: 101 us -> 101 us (level)
  no operation moved by 1% of the time
where the time goes in v6:
time: 101 us; the launch traced here: 100 us
  Pallas kernels  99.5 us (99%)
    pallas_call x1, Pallas kernels, exchange(): pl.pallas_call(kernel, out_shape=[jax.ShapeDtypeStruct(BLOCKS, F32)] * 3,...  97.4 us
    pallas_call x1, Pallas kernels, finish(): pl.pallas_call(finish_kernel, out_shape=[jax.ShapeDtypeStruct(w.shape, F3...  2.08 us

profile of v6, /device:TPU:32, one launch (start us, length us, event | category | flops | bytes accessed | tf_op | source)
XLA Modules:
  0.0 100.1 jit_solution(4350223022040804585)
XLA Ops:
  0.6 97.4 %exchange.1 = (f32[16,2,2,64,128]{4,3,2,1,0:T(8,128)S(1)}, f32[16,2,2,64,128]{4,3,2,1,0:T(8,128)S(1)}, f32[16,2,2,64,128]{4,3,2,1,0:T(8,128)S(1)}) custom-call(f32[16,2,2,64,128]{4,3,2,1,0:T(8,128)} %bitcast.31, f32[16,2,2,64,128]{4,3,2,1,0:T(8,128)} %bitcast.32, f32[16,2,2,64,128]{4,3,2,1,0:T(8,128)} %bitcast.33), custom_call_target="tpu_custom_call" | custom-call | tf_op jit(solution)/shard_map/exchange/pallas_call | solution.py:279
  98.0 2.1 %finish.1 = (f32[4096,128]{1,0:T(8,128)}, f32[4096,128]{1,0:T(8,128)}) custom-call(f32[4096,128]{1,0:T(8,128)S(1)} %bitcast.30, f32[4096,128]{1,0:T(8,128)S(1)} %bitcast.28, f32[4096,128]{1,0:T(8,128)S(1)} %bitcast.29), custom_call_target="tpu_custom_call" | custom-call | tf_op jit(solution)/shard_map/finish/pallas_call | solution.py:327

commit v7 on v6

--- a/solution.py
+++ b/solution.py
@@ -52,7 +52,7 @@
 def kernel(
     g_hbm, m_hbm, w_hbm, back, moved, held_w,
     gbuf, mbuf, D, R, X, G, GX, S, Z, QR, Y,
-    wsem, gsem, msem, p1s, p1r, xs, xr, zs, zr, qs, qr, p2s, p2r, ready,
+    wsem, insem, sent, p1r, xr, zr, qr, p2r, ready,
 ):
     s, m = lax.axis_index("shard"), lax.axis_index("model")
     zl, yy, core = s // 8, (s // 2) % 4, s % 2
@@ -63,8 +63,8 @@
     for q in range(4):
         c, r = 1 - q % 2, q // 2
         loads.append((
-            pltpu.make_async_copy(g_hbm.at[:, c, r], gbuf.at[q], gsem.at[q]),
-            pltpu.make_async_copy(m_hbm.at[:, c, r], mbuf.at[q], msem.at[q]),
+            pltpu.make_async_copy(g_hbm.at[:, c, r], gbuf.at[q], insem.at[q]),
+            pltpu.make_async_copy(m_hbm.at[:, c, r], mbuf.at[q], insem.at[q]),
         ))
 
     def load(q):
@@ -137,7 +137,7 @@
 
                 @pl.when(d != s)
                 def _():
-                    remote(rows, place, p1s.at[r], p1r.at[r], (d, m)).start()
+                    remote(rows, place, sent, p1r.at[r], (d, m)).start()
 
                 @pl.when(d == s)
                 def _():
@@ -174,7 +174,7 @@
 
             for k in range(1, 4):
                 q = (x + k) % 4
-                remote(G.at[r, q], GX.at[r, 3 - k], xs.at[r], xr.at[r], (s, zh * 4 + q)).start()
+                remote(G.at[r, q], GX.at[r, 3 - k], sent, xr.at[r], (s, zh * 4 + q)).start()
 
     def sum_step(r):
         with scope(f"xred#r={r}"):
@@ -185,11 +185,11 @@
                 def _():
                     pl.semaphore_wait(ready, 1)
 
-            remote(S.at[r], Z.at[r], zs.at[r], zr.at[r], partner).start()
+            remote(S.at[r], Z.at[r], sent, zr.at[r], partner).start()
 
     def chain_step(r):
         with scope(f"zred#r={r}"):
-            remote(S.at[r], Z.at[r], zs.at[r], zr.at[r], partner).wait_recv()
+            remote(S.at[r], Z.at[r], sent, zr.at[r], partner).wait_recv()
 
         with scope(f"chain#r={r}"):
             gram = S[r] + Z[r]
@@ -206,7 +206,7 @@
             QR[r, x] = (LINEAR**4 * eye + (LINEAR**2 * (early + late) + dot(late, early))) * scale
             for k in range(1, 4):
                 to = (s, zh * 4 + (x + k) % 4)
-                remote(QR.at[r, x], QR.at[r, x], qs.at[r], qr.at[r], to).start()
+                remote(QR.at[r, x], QR.at[r, x], sent, qr.at[r], to).start()
 
     def apply_step(r):
         with scope(f"qcast#r={r}"):
@@ -232,7 +232,7 @@
 
                     @pl.when(d != s)
                     def _():
-                        remote(rows, place, p2s.at[r], p2r.at[r], (d, m)).start()
+                        remote(rows, place, sent, p2r.at[r], (d, m)).start()
 
                     @pl.when(d == s)
                     def _():
@@ -257,14 +257,11 @@
     apply_step(1)
     with scope("sendwait"):
         pltpu.make_async_copy(w_hbm, held_w, wsem).wait()
-        for r in range(ROUNDS):
-            three = GX.at[r]
-            wait_bytes(three, xs.at[r])
-            wait_bytes(three, qs.at[r])
-            wait_bytes(S.at[r], zs.at[r])
-            for sem in (p1s, p2s):
-                wait_bytes(Y.at[r, pl.ds(0, 15)], sem.at[r])
-                wait_bytes(Y.at[r, 15, 0], sem.at[r])
+        for ref in (GX, GX, S):
+            wait_bytes(ref, sent)
+        for _ in range(2):
+            wait_bytes(Y.at[:, pl.ds(0, 15)], sent)
+            wait_bytes(Y.at[:, 15, 0], sent)
 
     for r in range(ROUNDS):
         with scope(f"p2wait#r={r}"):
@@ -291,8 +288,8 @@
             pltpu.VMEM((ROUNDS, *square), F32),
             pltpu.VMEM((ROUNDS, PER, *square), F32),
             moving,
-            dma(()), dma((4,)), dma((4,)),
-            *[dma((ROUNDS,))] * 10,
+            dma(()), dma((4,)), dma(()),
+            *[dma((ROUNDS,))] * 5,
             pltpu.SemaphoreType.REGULAR,
         ],
         compiler_params=pltpu.CompilerParams(
@@ -307,7 +304,6 @@
     momentum_out.start()
     pieces = 8
     size = w.shape[0] // pieces
-    outs = []
     for i in range(pieces):
         part = pl.ds(i * size, size)
 
@@ -316,10 +312,8 @@
             rows = pl.ds(pl.multiple_of(i * size + b * 128, 128), 128)
             held[rows, :] = w[rows, :] - learn_rate * back[rows, :]
 
-        outs.append(pltpu.make_async_copy(held.at[part], new_w.at[part], wsem.at[i]))
-        outs[-1].start()
-    for out in outs:
-        out.wait()
+        pltpu.make_async_copy(held.at[part], new_w.at[part], wsem).start()
+    pltpu.make_async_copy(held, new_w, wsem).wait()
     momentum_out.wait()
 
 
@@ -331,7 +325,7 @@
         out_specs=[pl.BlockSpec(memory_space=pltpu.HBM)] * 2,
         scratch_shapes=[
             pltpu.VMEM(w.shape, F32),
-            pltpu.SemaphoreType.DMA((8,)),
+            pltpu.SemaphoreType.DMA(()),
             pltpu.SemaphoreType.DMA(()),
         ],
         compiler_params=pltpu.CompilerParams(vmem_limit_bytes=16 * 1024 * 1024),

time: 101 us -> 101 us (level)
  no operation moved by 1% of the time
where the time goes in v7:
time: 101 us; the launch traced here: 99.9 us
  Pallas kernels  99.3 us (98%)
    pallas_call x1, Pallas kernels, exchange(): pl.pallas_call(kernel, out_shape=[jax.ShapeDtypeStruct(BLOCKS, F32)] * 3,...  97.3 us

profile of v7, /device:TPU:32, one launch (start us, length us, event | category | flops | bytes accessed | tf_op | source)
XLA Modules:
  0.0 99.9 jit_solution(5629994098353677583)
XLA Ops:
  0.6 97.3 %exchange.1 = (f32[16,2,2,64,128]{4,3,2,1,0:T(8,128)S(1)}, f32[16,2,2,64,128]{4,3,2,1,0:T(8,128)S(1)}, f32[16,2,2,64,128]{4,3,2,1,0:T(8,128)S(1)}) custom-call(f32[16,2,2,64,128]{4,3,2,1,0:T(8,128)} %bitcast.31, f32[16,2,2,64,128]{4,3,2,1,0:T(8,128)} %bitcast.32, f32[16,2,2,64,128]{4,3,2,1,0:T(8,128)} %bitcast.33), custom_call_target="tpu_custom_call" | custom-call | tf_op jit(solution)/shard_map/exchange/pallas_call | solution.py:276
  97.9 2.0 %finish.1 = (f32[4096,128]{1,0:T(8,128)}, f32[4096,128]{1,0:T(8,128)}) custom-call(f32[4096,128]{1,0:T(8,128)S(1)} %bitcast.30, f32[4096,128]{1,0:T(8,128)S(1)} %bitcast.28, f32[4096,128]{1,0:T(8,128)S(1)} %bitcast.29), custom_call_target="tpu_custom_call" | custom-call | tf_op jit(solution)/shard_map/finish/pallas_call | solution.py:321

commit v8 on v7

--- a/solution.py
+++ b/solution.py
@@ -52,7 +52,7 @@
 def kernel(
     g_hbm, m_hbm, w_hbm, back, moved, held_w,
     gbuf, mbuf, D, R, X, G, GX, S, Z, QR, Y,
-    wsem, insem, sent, p1r, xr, zr, qr, p2r, ready,
+    wsem, insem, sent, p1r, xr, zr, qr, p2r, ready, ready_x,
 ):
     s, m = lax.axis_index("shard"), lax.axis_index("model")
     zl, yy, core = s // 8, (s // 2) % 4, s % 2
@@ -86,9 +86,9 @@
         return z * 8 + ((yy + 2 + b) % 4) * 2 + c
 
     def late_dest(c, k):
-        half, a, b = k // 8, (k % 8) // 2, k % 2
+        a, half, b = k // 4, (k % 4) // 2, k % 2
         z = side * a + (1 - side) * (3 - a)
-        return z * 8 + (half * 2 + (yy + 1 + b) % 2) * 2 + c
+        return z * 8 + ((yy // 2 + 1 + half) % 2 * 2 + (yy + 1 + b) % 2) * 2 + c
 
     barrier = pltpu.get_barrier_semaphore()
 
@@ -101,8 +101,10 @@
             pl.semaphore_signal(barrier, inc=1, device_id=((s + k + i) % 32, m), device_id_type=MESH)
     for k in range(1, 8):
         pl.semaphore_signal(barrier, inc=1, device_id=((s + k) % 32, m), device_id_type=MESH)
-    for k in range(1, 4):
-        pl.semaphore_signal(barrier, inc=1, device_id=(s, zh * 4 + (x + k) % 4), device_id_type=MESH)
+    for q in range(1, 4):
+        @pl.when(x < q)
+        def _():
+            pl.semaphore_signal(barrier, inc=1, device_id=(s, zh * 4 + q), device_id_type=MESH)
 
 
     for q in range(4):
@@ -122,7 +124,12 @@
 
         if q == 0:
             with scope("barrier"):
-                pl.semaphore_wait(barrier, 34 + zh)
+                pl.semaphore_wait(barrier, 31 + x + zh)
+
+            for lower in range(3):
+                @pl.when(lower < x)
+                def _():
+                    pl.semaphore_signal(ready_x, inc=1, device_id=(s, zh * 4 + lower), device_id_type=MESH)
 
             @pl.when(zh == 1)
             def _():
@@ -171,6 +178,11 @@
                     X[r, j, :, 256 * h : 256 * h + 128] = low.reshape(128, 128)
                     X[r, j, :, 256 * h + 128 : 256 * h + 256] = high.reshape(128, 128)
                 G[r, j] = dot_t(X[r, j], X[r, j])
+
+            if r == 0:
+                @pl.when(x < 3)
+                def _():
+                    pl.semaphore_wait(ready_x, 3 - x)
 
             for k in range(1, 4):
                 q = (x + k) % 4
@@ -290,7 +302,7 @@
             moving,
             dma(()), dma((4,)), dma(()),
             *[dma((ROUNDS,))] * 5,
-            pltpu.SemaphoreType.REGULAR,
+            pltpu.SemaphoreType.REGULAR, pltpu.SemaphoreType.REGULAR,
         ],
         compiler_params=pltpu.CompilerParams(
             collective_id=0, has_side_effects=True, vmem_limit_bytes=40 * 1024 * 1024

time: 101 us -> 101 us (level)
  no operation moved by 1% of the time
where the time goes in v8:
time: 101 us
  Pallas kernels  100 us (99%)
    pallas_call x1, Pallas kernels, exchange(): pl.pallas_call(kernel, out_shape=[jax.ShapeDtypeStruct(BLOCKS, F32)] * 3,...  97.9 us

profile of v8, /device:TPU:32, one launch (start us, length us, event | category | flops | bytes accessed | tf_op | source)
XLA Modules:
  0.0 100.6 jit_solution(5783117528389315595)
XLA Ops:
  0.6 97.9 %exchange.1 = (f32[16,2,2,64,128]{4,3,2,1,0:T(8,128)S(1)}, f32[16,2,2,64,128]{4,3,2,1,0:T(8,128)S(1)}, f32[16,2,2,64,128]{4,3,2,1,0:T(8,128)S(1)}) custom-call(f32[16,2,2,64,128]{4,3,2,1,0:T(8,128)} %bitcast.31, f32[16,2,2,64,128]{4,3,2,1,0:T(8,128)} %bitcast.32, f32[16,2,2,64,128]{4,3,2,1,0:T(8,128)} %bitcast.33), custom_call_target="tpu_custom_call" | custom-call | tf_op jit(solution)/shard_map/exchange/pallas_call | solution.py:288
  98.6 2.0 %finish.1 = (f32[4096,128]{1,0:T(8,128)}, f32[4096,128]{1,0:T(8,128)}) custom-call(f32[4096,128]{1,0:T(8,128)S(1)} %bitcast.30, f32[4096,128]{1,0:T(8,128)S(1)} %bitcast.28, f32[4096,128]{1,0:T(8,128)S(1)} %bitcast.29), custom_call_target="tpu_custom_call" | custom-call | tf_op jit(solution)/shard_map/finish/pallas_call | solution.py:333

commit v9 on v8

--- a/solution.py
+++ b/solution.py
@@ -86,9 +86,9 @@
         return z * 8 + ((yy + 2 + b) % 4) * 2 + c
 
     def late_dest(c, k):
-        a, half, b = k // 4, (k % 4) // 2, k % 2
+        half, a, b = k // 8, (k % 8) // 2, k % 2
         z = side * a + (1 - side) * (3 - a)
-        return z * 8 + ((yy // 2 + 1 + half) % 2 * 2 + (yy + 1 + b) % 2) * 2 + c
+        return z * 8 + (half * 2 + (yy + 1 + b) % 2) * 2 + c
 
     barrier = pltpu.get_barrier_semaphore()
 

time: 101 us -> 101 us (level)
  no operation moved by 1% of the time
where the time goes in v9:
time: 101 us; the launch traced here: 99.9 us
  Pallas kernels  99.3 us (98%)
    pallas_call x1, Pallas kernels, exchange(): pl.pallas_call(kernel, out_shape=[jax.ShapeDtypeStruct(BLOCKS, F32)] * 3,...  97.2 us

profile of v9, /device:TPU:32, one launch (start us, length us, event | category | flops | bytes accessed | tf_op | source)
XLA Modules:
  0.0 99.9 jit_solution(7157325032240236249)
XLA Ops:
  0.6 97.2 %exchange.1 = (f32[16,2,2,64,128]{4,3,2,1,0:T(8,128)S(1)}, f32[16,2,2,64,128]{4,3,2,1,0:T(8,128)S(1)}, f32[16,2,2,64,128]{4,3,2,1,0:T(8,128)S(1)}) custom-call(f32[16,2,2,64,128]{4,3,2,1,0:T(8,128)} %bitcast.31, f32[16,2,2,64,128]{4,3,2,1,0:T(8,128)} %bitcast.32, f32[16,2,2,64,128]{4,3,2,1,0:T(8,128)} %bitcast.33), custom_call_target="tpu_custom_call" | custom-call | tf_op jit(solution)/shard_map/exchange/pallas_call | solution.py:288
  97.9 2.0 %finish.1 = (f32[4096,128]{1,0:T(8,128)}, f32[4096,128]{1,0:T(8,128)}) custom-call(f32[4096,128]{1,0:T(8,128)S(1)} %bitcast.30, f32[4096,128]{1,0:T(8,128)S(1)} %bitcast.28, f32[4096,128]{1,0:T(8,128)S(1)} %bitcast.29), custom_call_target="tpu_custom_call" | custom-call | tf_op jit(solution)/shard_map/finish/pallas_call | solution.py:333
